TPU v7x, 32 devices: a whole 2x2x4 slice. The times are simulated.
32 devices in a mesh: ctx: 8 (over z, y), mp: 4 (over x, core).
Axes of the slice: x: 2, y: 2, z: 4, core: 2. Of those that a mesh axis runs over, the one named last changes fastest.
Arguments:
- queries: bfloat16 [2048, 4096], P('ctx', 'mp'), may hold values from -20 to 20
- keys: bfloat16 [2048, 2048], P('ctx', 'mp'), may hold values from -20 to 20
- values: bfloat16 [2048, 2048], P('ctx', 'mp'), may hold values from -6 to 6
- out_grad: bfloat16 [2048, 4608], P('ctx', 'mp'), may hold values from -6 to 6
- doc_ids: int32 [2048], P('ctx'), may hold values from 0 to 7, never falling along the last dimension, each value on 1 to 768 neighbouring positions
- w_out: bfloat16 [4096, 4608], P('mp'), may hold values from -0.09375 to 0.09375
Outputs:
- query_gradient: bfloat16 [2048, 4096], P('ctx', 'mp')
- key_gradient: bfloat16 [2048, 2048], P('ctx', 'mp')
- value_gradient: bfloat16 [2048, 2048], P('ctx', 'mp')
Inputs may be any that keep to these rules, and one draw needn't show every extreme that they name: `doc_ids`: document numbers never fall along the sequence; every document has at most (3) * 256 tokens, and some document has exactly that many.
All inputs are finite; a program needn't handle non-finite values.
Results may differ from a plain program's by a relative error of at most 0.0069.
Values may be sent and summed in bfloat16 or wider, within the bound.
A program may use at most 64 MiB of HBM per device.

v0:
```python
import jax
import jax.numpy as jnp
from jax import lax
from jax.sharding import PartitionSpec as P

QUERY_HEADS = 32
KEY_VALUE_HEADS = 16
HEAD_SIZE = 128
SPAN = 4


cap_value = 50.0
query_scale = 1.0 / 12.0


def passed_along(value, axis, steps):
    count = lax.axis_size(axis)
    first, last = (max(0, -steps), min(count, count - steps))
    return lax.ppermute(value, axis, [(source, source + steps) for source in range(first, last)])


def body(queries, keys, values, out_grad, doc_ids, w_out):
    rows = queries.shape[0]
    kv_heads = keys.shape[1] // HEAD_SIZE
    query_groups = QUERY_HEADS // KEY_VALUE_HEADS
    here = lax.axis_index("ctx")
    id_blocks = [doc_ids]
    ids_now = doc_ids
    for hop in range(1, SPAN):
        ids_now = passed_along(ids_now, "ctx", 1)
        id_blocks.append(ids_now)
    incoming_gradient = lax.dot_general(
        lax.all_gather(out_grad, "mp", axis=1, tiled=True),
        w_out,
        (((1,), (1,)), ((), ())),
        preferred_element_type=jnp.float32,
    ).astype(jnp.bfloat16)
    query_quad = queries.reshape(rows, kv_heads, query_groups, HEAD_SIZE)
    gradient_quad = incoming_gradient.reshape(rows, kv_heads, query_groups, HEAD_SIZE)
    offsets = jnp.arange(rows, dtype=jnp.int32)
    query_pos = here * rows + offsets

    def key_mask(hop):
        source = here - hop
        key_ids = id_blocks[hop]
        key_pos = source * rows + offsets
        mask = (
            (doc_ids[:, None] == key_ids[None, :])
            & (key_pos[None, :] <= query_pos[:, None])
            & (source >= 0)
        )
        if hop == 0:
            touched = jnp.array(True)
        else:
            touched = (source >= 0) & (key_ids[rows - 1] == doc_ids[0])
        return (mask, touched)

    def capped(key_slab):
        raw = jnp.einsum("qhgd,khd->hgqk", query_quad, key_slab, preferred_element_type=jnp.float32)
        tanh_part = jnp.tanh(raw * (query_scale / cap_value))
        return (cap_value * tanh_part, tanh_part)

    current = jnp.stack([keys, values])
    blocks = [current]
    for hop in range(1, SPAN):
        current = passed_along(current, "ctx", 1)
        blocks.append(current)
    masks = [key_mask(hop) for hop in range(SPAN)]
    weight_sum = jnp.zeros((kv_heads, query_groups, rows), jnp.float32)
    value_sum = jnp.zeros((rows, kv_heads, query_groups, HEAD_SIZE), jnp.float32)
    for hop in range(SPAN):

        def forward_tile(
            key_slab=blocks[hop][0].reshape(rows, kv_heads, HEAD_SIZE),
            value_slab=blocks[hop][1].reshape(rows, kv_heads, HEAD_SIZE),
            mask=masks[hop][0],
        ):
            scores, tanh_part = capped(key_slab)
            weights = jnp.where(mask, jnp.exp(scores), 0.0)
            return (
                jnp.sum(weights, axis=3),
                jnp.einsum(
                    "hgqk,khd->qhgd",
                    weights.astype(jnp.bfloat16),
                    value_slab,
                    preferred_element_type=jnp.float32,
                ),
            )

        weight_part, value_portion = forward_tile()
        weight_sum = weight_sum + weight_part
        value_sum = value_sum + value_portion
    logsum_total = jnp.log(weight_sum)
    attended = value_sum / jnp.transpose(weight_sum, (2, 0, 1))[..., None]
    row_correction = jnp.transpose(
        jnp.sum(gradient_quad.astype(jnp.float32) * attended, axis=3), (1, 2, 0)
    )

    def run_back(hop):

        def backward_tile(
            key_slab=blocks[hop][0].reshape(rows, kv_heads, HEAD_SIZE),
            value_slab=blocks[hop][1].reshape(rows, kv_heads, HEAD_SIZE),
            mask=masks[hop][0],
        ):
            scores, tanh_part = capped(key_slab)
            probs = jnp.where(mask, jnp.exp(scores - logsum_total[..., None]), 0.0)
            prob_grad = jnp.einsum(
                "qhgd,khd->hgqk", gradient_quad, value_slab, preferred_element_type=jnp.float32
            )
            logit_grad = (
                probs
                * (prob_grad - row_correction[..., None])
                * (1.0 - tanh_part * tanh_part)
                * query_scale
            ).astype(jnp.bfloat16)
            query_part = jnp.einsum(
                "hgqk,khd->qhgd", logit_grad, key_slab, preferred_element_type=jnp.float32
            )
            key_portion = jnp.einsum(
                "hgqk,qhgd->khd", logit_grad, query_quad, preferred_element_type=jnp.float32
            )
            value_portion = jnp.einsum(
                "hgqk,qhgd->khd",
                probs.astype(jnp.bfloat16),
                gradient_quad,
                preferred_element_type=jnp.float32,
            )
            return (
                query_part,
                jnp.stack(
                    [
                        key_portion.reshape(rows, kv_heads * HEAD_SIZE),
                        value_portion.reshape(rows, kv_heads * HEAD_SIZE),
                    ]
                ),
            )

        return backward_tile()

    query_part, key_value_total = run_back(0)
    query_total = query_part
    for hop in range(1, SPAN):
        query_part, key_value_part = run_back(hop)
        query_total = query_total + query_part
        key_value_total = key_value_total + passed_along(
            key_value_part.astype(jnp.bfloat16), "ctx", -hop
        ).astype(key_value_part.dtype)
    return (
        query_total.reshape(rows, kv_heads * query_groups * HEAD_SIZE).astype(jnp.bfloat16),
        key_value_total[0].astype(jnp.bfloat16),
        key_value_total[1].astype(jnp.bfloat16),
    )


def solution(mesh):
    placed = (
        P("ctx", "mp"),
        P("ctx", "mp"),
        P("ctx", "mp"),
        P("ctx", "mp"),
        P("ctx"),
        P("mp", None),
    )
    return jax.shard_map(
        body,
        mesh=mesh,
        in_specs=placed,
        out_specs=(P("ctx", "mp"), P("ctx", "mp"), P("ctx", "mp")),
        check_vma=False,
    )
```

profile of v0, /device:TPU:6, one launch (start us, length us, event | category | flops | bytes accessed | tf_op | source)
XLA Modules:
  0.0 155.7 jit_solution(16597687430622721278)
XLA Ops:
  7.2 3.6 %collective-permute-start = (s32[256]{0:T(256)}, s32[256]{0:T(256)S(1)}, u32[]{:S(2)}, u32[]{:S(2)}) collective-permute-start(s32[256]{0:T(256)} %param.10), channel_id=1, source_target_pairs={{0,4},{4,8},{8,12},{12,16},{16,20},{20,24},{24,28},{1,5},{5,9},{9,... | collective-permute-start | bytes 3080 | tf_op jit(solution)/shard_map/ppermute | solution.py:19
  13.1 3.4 %collective-permute-start.1 = (bf16[2,256,512]{1,2,0:T(8,128)(2,1)S(1)}, bf16[2,256,512]{1,2,0:T(8,128)(2,1)}, u32[]{:S(2)}, u32[]{:S(2)}) collective-permute-start(bf16[2,256,512]{1,2,0:T(8,128)(2,1)S(1)} %pad_maximum_fusion), channel_id=1, source_target_pairs={{0,4},{4,8},{8,12},{12,16},{16,20},{20,24},{24,28},{1,5},{5,9},{9,... | collective-permute-start | bytes 1572872 | tf_op jit(solution)/shard_map/ppermute | solution.py:19
  16.5 3.4 %collective-permute-start.2 = (s32[256]{0:T(256)S(1)}, s32[256]{0:T(256)S(1)}, u32[]{:S(2)}, u32[]{:S(2)}) collective-permute-start(s32[256]{0:T(256)S(1)} %collective-permute-done), channel_id=1, source_target_pairs={{0,4},{4,8},{8,12},{12,16},{16,20},{20,24},{24,28},{1,5},{5,9},{9,... | collective-permute-start | bytes 3080 | tf_op jit(solution)/shard_map/ppermute | solution.py:19
  20.0 8.5 %collective-permute-done.2 = s32[256]{0:T(256)S(1)} collective-permute-done((s32[256]{0:T(256)S(1)}, s32[256]{0:T(256)S(1)}, u32[]{:S(2)}, u32[]{:S(2)}) %collective-permute-start.2) | collective-permute-done | bytes 1056 | tf_op jit(solution)/shard_map/ppermute | solution.py:19
  28.5 4.3 %collective-permute-start.4 = (s32[256]{0:T(256)S(1)}, s32[256]{0:T(256)S(1)}, u32[]{:S(2)}, u32[]{:S(2)}) collective-permute-start(s32[256]{0:T(256)S(1)} %collective-permute-done.2), channel_id=1, source_target_pairs={{0,4},{4,8},{8,12},{12,16},{16,20},{20,24},{24,28},{1,5},{5,9},{9,... | collective-permute-start | bytes 3080 | tf_op jit(solution)/shard_map/ppermute | solution.py:19
  35.9 5.1 %collective-permute-start.3 = (bf16[2,256,512]{1,2,0:T(8,128)(2,1)}, bf16[2,256,512]{1,2,0:T(8,128)(2,1)S(1)}, u32[]{:S(2)}, u32[]{:S(2)}) collective-permute-start(bf16[2,256,512]{1,2,0:T(8,128)(2,1)} %collective-permute-done.1), channel_id=1, source_target_pairs={{0,4},{4,8},{8,12},{12,16},{16,20},{20,24},{24,28},{1,5},{5,9},{9,... | collective-permute-start | bytes 1572872 | tf_op jit(solution)/shard_map/ppermute | solution.py:19
  43.5 6.8 %collective-permute-done.3 = bf16[2,256,512]{1,2,0:T(8,128)(2,1)S(1)} collective-permute-done((bf16[2,256,512]{1,2,0:T(8,128)(2,1)}, bf16[2,256,512]{1,2,0:T(8,128)(2,1)S(1)}, u32[]{:S(2)}, u32[]{:S(2)}) %collective-permute-start.3) | collective-permute-done | bytes 524320 | tf_op jit(solution)/shard_map/ppermute | solution.py:19
  50.3 5.4 %collective-permute-start.5 = (bf16[2,256,512]{1,2,0:T(8,128)(2,1)S(1)}, bf16[2,256,512]{1,2,0:T(8,128)(2,1)S(1)}, u32[]{:S(2)}, u32[]{:S(2)}) collective-permute-start(bf16[2,256,512]{1,2,0:T(8,128)(2,1)S(1)} %collective-permute-done.3), channel_id=1, source_target_pairs={{0,4},{4,8},{8,12},{12,16},{16,20},{20,24},{24,28},{1,5},{5,9},{9,... | collective-permute-start | bytes 1572872 | tf_op jit(solution)/shard_map/ppermute | solution.py:19
  57.2 1.6 %fusion.37 = f32[256,4,2,128]{0,3,2,1:T(8,128)} fusion(f32[256,4,2,128]{0,3,2,1:T(8,128)S(1)} %fusion.36, bf16[256,4,128,1]{0,2,3,1:T(8,128)(2,1)S(1)} %bitcast.346, f32[4,256,256,2]{2,1,3,0:T(8,128)S(1)} %get-tuple-element.26, pred[256,256]{0,1:T(8,128)(4,1)S(1)} %get-tuple-element.20), kind=kOutput, calls=%fused_computation.65 | convolution fusion | flops 136052736 | bytes 4521984 | tf_op jit(solution)/shard_map/hgqk,khd->qhgd/dot_general | solution.py:82
  58.8 4.7 %collective-permute-done.5 = bf16[2,256,512]{1,2,0:T(8,128)(2,1)S(1)} collective-permute-done((bf16[2,256,512]{1,2,0:T(8,128)(2,1)S(1)}, bf16[2,256,512]{1,2,0:T(8,128)(2,1)S(1)}, u32[]{:S(2)}, u32[]{:S(2)}) %collective-permute-start.5) | collective-permute-done | bytes 524320 | tf_op jit(solution)/shard_map/ppermute | solution.py:19
  65.0 2.2 %fusion.35 = (f32[4,2,256]{2,1,0:T(2,128)S(1)}, f32[4,256,256,2]{2,1,3,0:T(8,128)}) fusion(pred[256,256]{0,1:T(8,128)(4,1)S(1)} %get-tuple-element.19, bf16[256,4,128,1]{0,2,3,1:T(8,128)(2,1)S(1)} %bitcast.356, bf16[256,4,2,128]{0,3,2,1:T(8,128)(2,1)S(1)} %bitcast.334), kind=kOutput, calls=%fused_computation.55 | convolution fusion | flops 136312832 | bytes 2957312 | tf_op jit(solution)/shard_map/qhgd,khd->hgqk/dot_general | solution.py:59
  67.2 7.8 %convolution_convert_fusion = bf16[256,1024]{1,0:T(8,128)(2,1)} fusion(bf16[256,4608]{1,0:T(8,128)(2,1)} %all-gather.2.cloned.1.call-done, bf16[1024,4608]{1,0:T(8,128)(2,1)} %param.11), kind=kOutput, calls=%fused_computation.72 | convolution fusion | flops 2416181248 | bytes 12320768 | tf_op jit(solution)/shard_map/dot_general | solution.py:32
  75.1 2.0 %copy.182 = bf16[256,1024]{0,1:T(8,128)(2,1)} copy(bf16[256,1024]{1,0:T(8,128)(2,1)} %convolution_convert_fusion) | data formatting | bytes 1048576 | tf_op jit(solution)/shard_map/reshape | solution.py:39
  77.1 2.5 %fusion.47 = bf16[4,128,256]{2,1,0:T(8,128)(2,1)} fusion(bf16[256,4,2,128]{0,3,2,1:T(8,128)(2,1)} %bitcast.359, f32[4,256,256,2]{2,1,3,0:T(8,128)S(1)} %get-tuple-element.30, f32[4,2,256]{2,1,0:T(2,128)S(1)} %bitcast.375, pred[256,256]{0,1:T(8,128)(4,1)S(1)} %get-tuple-element.22), kind=kOutput, calls=%fused_computation.82 | convolution fusion | flops 136445952 | bytes 2957312 | tf_op jit(solution)/shard_map/hgqk,qhgd->khd/dot_general | solution.py:123
  79.6 1.3 fusion.49
  85.3 2.0 %fusion.1 = bf16[4,2,256,256]{2,3,1,0:T(8,128)(2,1)} fusion(f32[4,256,256,2]{2,1,3,0:T(8,128)S(1)} %copy-done.27, bf16[256,4,128,1]{0,2,3,1:T(8,128)(2,1)S(1)} %bitcast.372, bf16[256,4,2,128]{0,3,2,1:T(8,128)(2,1)S(1)} %bitcast.364, f32[4,2,256]{2,1,0:T(2,128)S(1)} %bitcast.388, f32[4,2,256]{2,1,0:T(2,128)S(1)} %bitcast.379, pred[256,256]{0,1:T(8,128)(4,1)S(1)} %copy-done.25), kind=kOutput, calls=%fused_computation.2 | convolution fusion | flops 139460608 | bytes 4014080 | tf_op jit(solution)/shard_map/qhgd,khd->hgqk/dot_general | solution.py:108
  87.3 1.3 fusion.51
  89.0 1.4 fusion.56
  91.9 1.3 convolution_bitcast_fusion
  93.1 1.8 %copy.106 = bf16[1,256,512]{2,1,0:T(8,128)(2,1)} copy(bf16[1,256,512]{1,2,0:T(8,128)(2,1)} %bitcast.370) | data formatting | bytes 524288 | tf_op jit(solution)/shard_map/stack;reshape | solution.py:131
  96.3 1.9 %pad_maximum_fusion.1 = bf16[2,256,512]{2,1,0:T(8,128)(2,1)} fusion(bf16[1,256,512]{2,1,0:T(8,128)(2,1)} %copy.106, bf16[1,256,512]{2,1,0:T(8,128)(2,1)} %copy.105), kind=kLoop, calls=%fused_computation.121 | loop fusion | flops 262144 | bytes 1048576 | tf_op jit(solution)/shard_map/stack | solution.py:131
  98.1 1.9 %collective-permute-start.6 = (bf16[2,256,512]{2,1,0:T(8,128)(2,1)}, bf16[2,256,512]{2,1,0:T(8,128)(2,1)}, u32[]{:S(2)}, u32[]{:S(2)}) collective-permute-start(bf16[2,256,512]{2,1,0:T(8,128)(2,1)} %pad_maximum_fusion.1), channel_id=1, source_target_pairs={{4,0},{8,4},{12,8},{16,12},{20,16},{24,20},{28,24},{5,1},{9,5},{13... | collective-permute-start | bytes 1572872 | tf_op jit(solution)/shard_map/ppermute | solution.py:19
  100.0 1.8 %copy.112 = bf16[1,256,512]{2,1,0:T(8,128)(2,1)} copy(bf16[1,256,512]{1,2,0:T(8,128)(2,1)} %bitcast.368) | data formatting | bytes 524288 | tf_op jit(solution)/shard_map/stack;reshape | solution.py:131
  103.2 1.9 %pad_maximum_fusion.2 = bf16[2,256,512]{2,1,0:T(8,128)(2,1)} fusion(bf16[1,256,512]{2,1,0:T(8,128)(2,1)} %copy.112, bf16[1,256,512]{2,1,0:T(8,128)(2,1)} %copy.111), kind=kLoop, calls=%fused_computation.122 | loop fusion | flops 262144 | bytes 1048576 | tf_op jit(solution)/shard_map/stack | solution.py:131
  105.0 1.5 collective-permute-start.7
  106.5 1.7 %fusion.50 = bf16[4,256,128]{1,2,0:T(8,128)(2,1)S(1)} fusion(bf16[4,2,256,256]{2,3,1,0:T(8,128)(2,1)} %fusion.1, bf16[256,4,2,128]{0,3,2,1:T(8,128)(2,1)S(1)} %bitcast.338), kind=kOutput, calls=%fused_computation.85 | convolution fusion | flops 134348800 | bytes 1835008 | tf_op jit(solution)/shard_map/hgqk,qhgd->khd/dot_general | solution.py:120
  110.4 1.3 collective-permute-start.8
  111.7 1.2 copy.100
  113.9 1.6 %fusion.41 = f32[256,4,2,128]{0,3,2,1:T(8,128)S(1)} fusion(f32[256,4,2,128]{0,3,2,1:T(8,128)} %convolution_bitcast_fusion, bf16[256,4,128,1]{0,2,3,1:T(8,128)(2,1)S(1)} %bitcast.353, bf16[4,2,256,256]{2,3,1,0:T(8,128)(2,1)S(1)} %fusion.7), kind=kOutput, calls=%fused_computation.69 | convolution fusion | flops 134479872 | bytes 3407872 | tf_op jit(solution)/shard_map/hgqk,khd->qhgd/dot_general | solution.py:117
  118.1 6.1 %collective-permute-done.7 = bf16[2,256,512]{2,1,0:T(8,128)(2,1)} collective-permute-done((bf16[2,256,512]{2,1,0:T(8,128)(2,1)}, bf16[2,256,512]{2,1,0:T(8,128)(2,1)}, u32[]{:S(2)}, u32[]{:S(2)}) %collective-permute-start.7) | collective-permute-done | bytes 524320 | tf_op jit(solution)/shard_map/ppermute | solution.py:19
  124.2 22.2 %collective-permute-done.8 = bf16[2,256,512]{2,1,0:T(8,128)(2,1)} collective-permute-done((bf16[2,256,512]{2,1,0:T(8,128)(2,1)}, bf16[2,256,512]{2,1,0:T(8,128)(2,1)}, u32[]{:S(2)}, u32[]{:S(2)}) %collective-permute-start.8) | collective-permute-done | bytes 524320 | tf_op jit(solution)/shard_map/ppermute | solution.py:19
  146.4 1.6 %fusion.63 = bf16[2,256,512]{2,1,0:T(8,128)(2,1)S(1)} fusion(f32[1,256,512]{2,1,0:T(8,128)S(1)} %copy.100, f32[1,256,512]{2,1,0:T(8,128)S(1)} %copy-done.7, bf16[2,256,512]{2,1,0:T(8,128)(2,1)} %collective-permute-done.8, bf16[2,256,512]{2,1,0:T(8,128)(2,1)} %collective-permute-done.7, bf16[2,256,512]{2,1,0:T(8,128)(2,1)} %collective-permute-done.6), kind=kLoop, calls=%fused_computation.91 | loop fusion | flops 2097152 | bytes 3145728 | tf_op jit(solution)/shard_map/convert.1
  (100 shorter events, 26.2 us)
Async XLA Ops:
  7.2 25.6 %copy-start.9 = (bf16[256,512]{1,0:T(8,128)(2,1)S(1)}, bf16[256,512]{1,0:T(8,128)(2,1)}, u32[]{:S(2)}) copy-start(bf16[256,512]{1,0:T(8,128)(2,1)} %param.7) | copy-start | bytes 786436
  7.2 25.7 %copy-start.10 = (bf16[256,512]{1,0:T(8,128)(2,1)S(1)}, bf16[256,512]{1,0:T(8,128)(2,1)}, u32[]{:S(2)}) copy-start(bf16[256,512]{1,0:T(8,128)(2,1)} %param.8) | copy-start | bytes 786436
  7.2 25.8 %copy-start.19 = (bf16[256,1024]{1,0:T(8,128)(2,1)S(1)}, bf16[256,1024]{1,0:T(8,128)(2,1)}, u32[]{:S(2)}) copy-start(bf16[256,1024]{1,0:T(8,128)(2,1)} %param.6) | copy-start | bytes 1572868
  7.2 60.0 %all-gather.2.cloned.1.call-start = ((), (), s32[]{:S(2)}) async-start(), calls=%async_computation | async-start | bytes 2949120 | tf_op jit(solution)/shard_map/all_gather | solution.py:33
  7.2 9.3 %collective-permute-start = (s32[256]{0:T(256)}, s32[256]{0:T(256)S(1)}, u32[]{:S(2)}, u32[]{:S(2)}) collective-permute-start(s32[256]{0:T(256)} %param.10), channel_id=1, source_target_pairs={{0,4},{4,8},{8,12},{12,16},{16,20},{20,24},{24,28},{1,5},{5,9},{9,... | collective-permute-start | bytes 3080 | tf_op jit(solution)/shard_map/ppermute | solution.py:19
  13.0 21.0 %copy-start.26 = (s32[256]{0:T(256)S(1)}, s32[256]{0:T(256)}, u32[]{:S(2)}) copy-start(s32[256]{0:T(256)} %param.10) | copy-start | bytes 3076
  13.1 22.9 %collective-permute-start.1 = (bf16[2,256,512]{1,2,0:T(8,128)(2,1)S(1)}, bf16[2,256,512]{1,2,0:T(8,128)(2,1)}, u32[]{:S(2)}, u32[]{:S(2)}) collective-permute-start(bf16[2,256,512]{1,2,0:T(8,128)(2,1)S(1)} %pad_maximum_fusion), channel_id=1, source_target_pairs={{0,4},{4,8},{8,12},{12,16},{16,20},{20,24},{24,28},{1,5},{5,9},{9,... | collective-permute-start | bytes 1572872 | tf_op jit(solution)/shard_map/ppermute | solution.py:19
  16.5 11.9 %collective-permute-start.2 = (s32[256]{0:T(256)S(1)}, s32[256]{0:T(256)S(1)}, u32[]{:S(2)}, u32[]{:S(2)}) collective-permute-start(s32[256]{0:T(256)S(1)} %collective-permute-done), channel_id=1, source_target_pairs={{0,4},{4,8},{8,12},{12,16},{16,20},{20,24},{24,28},{1,5},{5,9},{9,... | collective-permute-start | bytes 3080 | tf_op jit(solution)/shard_map/ppermute | solution.py:19
  28.5 5.6 %collective-permute-start.4 = (s32[256]{0:T(256)S(1)}, s32[256]{0:T(256)S(1)}, u32[]{:S(2)}, u32[]{:S(2)}) collective-permute-start(s32[256]{0:T(256)S(1)} %collective-permute-done.2), channel_id=1, source_target_pairs={{0,4},{4,8},{8,12},{12,16},{16,20},{20,24},{24,28},{1,5},{5,9},{9,... | collective-permute-start | bytes 3080 | tf_op jit(solution)/shard_map/ppermute | solution.py:19
  33.5 1.8 %copy-start.11 = (bf16[256,4,128,1]{0,2,3,1:T(8,128)(2,1)}, bf16[256,4,128,1]{0,2,3,1:T(8,128)(2,1)S(1)}, u32[]{:S(2)}) copy-start(bf16[256,4,128,1]{0,2,3,1:T(8,128)(2,1)S(1)} %copy.127) | copy-start | bytes 786436
  34.5 1.4 copy-start.21
  34.5 29.7 %copy-start.24 = (pred[256,256]{0,1:T(8,128)(4,1)}, pred[256,256]{0,1:T(8,128)(4,1)S(1)}, u32[]{:S(2)}) copy-start(pred[256,256]{0,1:T(8,128)(4,1)S(1)} %get-tuple-element.19) | copy-start | bytes 196612
  35.4 6.7 %copy-start.1 = (f32[4,256,256,2]{2,1,3,0:T(8,128)}, f32[4,256,256,2]{2,1,3,0:T(8,128)S(1)}, u32[]{:S(2)}) copy-start(f32[4,256,256,2]{2,1,3,0:T(8,128)S(1)} %get-tuple-element.28) | copy-start | bytes 6291460
  35.9 14.3 %collective-permute-start.3 = (bf16[2,256,512]{1,2,0:T(8,128)(2,1)}, bf16[2,256,512]{1,2,0:T(8,128)(2,1)S(1)}, u32[]{:S(2)}, u32[]{:S(2)}) collective-permute-start(bf16[2,256,512]{1,2,0:T(8,128)(2,1)} %collective-permute-done.1), channel_id=1, source_target_pairs={{0,4},{4,8},{8,12},{12,16},{16,20},{20,24},{24,28},{1,5},{5,9},{9,... | collective-permute-start | bytes 1572872 | tf_op jit(solution)/shard_map/ppermute | solution.py:19
  42.1 1.4 copy-start.13
  42.9 34.2 %copy-start.3 = (f32[4,256,256,2]{2,1,3,0:T(8,128)}, f32[4,256,256,2]{2,1,3,0:T(8,128)S(1)}, u32[]{:S(2)}) copy-start(f32[4,256,256,2]{2,1,3,0:T(8,128)S(1)} %get-tuple-element.30) | copy-start | bytes 6291460
  50.3 13.3 %collective-permute-start.5 = (bf16[2,256,512]{1,2,0:T(8,128)(2,1)S(1)}, bf16[2,256,512]{1,2,0:T(8,128)(2,1)S(1)}, u32[]{:S(2)}, u32[]{:S(2)}) collective-permute-start(bf16[2,256,512]{1,2,0:T(8,128)(2,1)S(1)} %collective-permute-done.3), channel_id=1, source_target_pairs={{0,4},{4,8},{8,12},{12,16},{16,20},{20,24},{24,28},{1,5},{5,9},{9,... | collective-permute-start | bytes 1572872 | tf_op jit(solution)/shard_map/ppermute | solution.py:19
  57.2 1.6 %copy-start.5 = (f32[4,256,256,2]{2,1,3,0:T(8,128)}, f32[4,256,256,2]{2,1,3,0:T(8,128)S(1)}, u32[]{:S(2)}) copy-start(f32[4,256,256,2]{2,1,3,0:T(8,128)S(1)} %get-tuple-element.26) | copy-start | bytes 6291460
  77.1 2.5 %copy-start.6 = (f32[4,256,256,2]{2,1,3,0:T(8,128)S(1)}, f32[4,256,256,2]{2,1,3,0:T(8,128)}, u32[]{:S(2)}) copy-start(f32[4,256,256,2]{2,1,3,0:T(8,128)} %copy-done.5) | copy-start | bytes 6291460
  77.1 2.5 %copy-start.20 = (bf16[256,1024]{0,1:T(8,128)(2,1)S(1)}, bf16[256,1024]{0,1:T(8,128)(2,1)}, u32[]{:S(2)}) copy-start(bf16[256,1024]{0,1:T(8,128)(2,1)} %copy.182) | copy-start | bytes 1572868
  79.6 1.3 copy-start.23
  79.6 2.1 %copy-start.27 = (f32[4,256,256,2]{2,1,3,0:T(8,128)S(1)}, f32[4,256,256,2]{2,1,3,0:T(8,128)}, u32[]{:S(2)}) copy-start(f32[4,256,256,2]{2,1,3,0:T(8,128)} %get-tuple-element.24) | copy-start | bytes 6291460
  81.7 1.6 %copy-start.4 = (f32[4,256,256,2]{2,1,3,0:T(8,128)S(1)}, f32[4,256,256,2]{2,1,3,0:T(8,128)}, u32[]{:S(2)}) copy-start(f32[4,256,256,2]{2,1,3,0:T(8,128)} %copy-done.3) | copy-start | bytes 6291460
  87.3 1.7 %copy-start.2 = (f32[4,256,256,2]{2,1,3,0:T(8,128)S(1)}, f32[4,256,256,2]{2,1,3,0:T(8,128)}, u32[]{:S(2)}) copy-start(f32[4,256,256,2]{2,1,3,0:T(8,128)} %copy-done.1) | copy-start | bytes 6291460
  87.3 1.7 %copy-start.22 = (pred[256,256]{0,1:T(8,128)(4,1)S(1)}, pred[256,256]{0,1:T(8,128)(4,1)}, u32[]{:S(2)}) copy-start(pred[256,256]{0,1:T(8,128)(4,1)} %copy-done.21) | copy-start | bytes 196612
  89.0 1.4 copy-start.12
  98.1 20.0 %collective-permute-start.6 = (bf16[2,256,512]{2,1,0:T(8,128)(2,1)}, bf16[2,256,512]{2,1,0:T(8,128)(2,1)}, u32[]{:S(2)}, u32[]{:S(2)}) collective-permute-start(bf16[2,256,512]{2,1,0:T(8,128)(2,1)} %pad_maximum_fusion.1), channel_id=1, source_target_pairs={{4,0},{8,4},{12,8},{16,12},{20,16},{24,20},{28,24},{5,1},{9,5},{13... | collective-permute-start | bytes 1572872 | tf_op jit(solution)/shard_map/ppermute | solution.py:19
  105.0 19.1 %collective-permute-start.7 = (bf16[2,256,512]{2,1,0:T(8,128)(2,1)}, bf16[2,256,512]{2,1,0:T(8,128)(2,1)}, u32[]{:S(2)}, u32[]{:S(2)}) collective-permute-start(bf16[2,256,512]{2,1,0:T(8,128)(2,1)} %pad_maximum_fusion.2), channel_id=1, source_target_pairs={{8,0},{12,4},{16,8},{20,12},{24,16},{28,20},{9,1},{13,5},{17,9},{2... | collective-permute-start | bytes 1572872 | tf_op jit(solution)/shard_map/ppermute | solution.py:19
  108.4 5.5 %copy-start.14 = (bf16[1,256,512]{1,2,0:T(8,128)(2,1)S(1)}, bf16[1,256,512]{1,2,0:T(8,128)(2,1)}, u32[]{:S(2)}) copy-start(bf16[1,256,512]{1,2,0:T(8,128)(2,1)} %copy-done.13) | copy-start | bytes 786436
  110.4 36.0 %collective-permute-start.8 = (bf16[2,256,512]{2,1,0:T(8,128)(2,1)}, bf16[2,256,512]{2,1,0:T(8,128)(2,1)}, u32[]{:S(2)}, u32[]{:S(2)}) collective-permute-start(bf16[2,256,512]{2,1,0:T(8,128)(2,1)} %pad_maximum_fusion.3), channel_id=1, source_target_pairs={{12,0},{16,4},{20,8},{24,12},{28,16},{13,1},{17,5},{21,9},{25,13},... | collective-permute-start | bytes 1572872 | tf_op jit(solution)/shard_map/ppermute | solution.py:19
  113.9 1.6 %copy-start.16 = (bf16[1,256,512]{1,2,0:T(8,128)(2,1)S(1)}, bf16[1,256,512]{1,2,0:T(8,128)(2,1)}, u32[]{:S(2)}) copy-start(bf16[1,256,512]{1,2,0:T(8,128)(2,1)} %copy-done.15) | copy-start | bytes 786436
  116.8 29.6 %copy-start.7 = (f32[1,256,512]{2,1,0:T(8,128)S(1)}, f32[1,256,512]{2,1,0:T(8,128)}, u32[]{:S(2)}) copy-start(f32[1,256,512]{2,1,0:T(8,128)} %copy.99) | copy-start | bytes 1572868
  (6 other events, 6.6 us)
Sparse Core Ops, SparseCore 0:
  16.6 23.2 all-gather.1
where the time goes:
time: 157 us; the launch traced here: 156 us
  waiting for transfers between devices  48.8 us (31%)
  matrix products  33.7 us (21%)
  starting transfers between devices  29.9 us (19%)
  local copies, waits for them, and re-layouts  21.9 us (14%)
  between operations  14.6 us (9%)
  other arithmetic  6.78 us (4%)
    ppermute x9, waiting for transfers between devices, passed_along(): lax.ppermute(value, axis, [(source, source + steps) for source in range(f...  48.8 us
    ppermute x9, starting transfers between devices, passed_along(): lax.ppermute(value, axis, [(source, source + steps) for source in range(f...  29.9 us
    another operation x8, local copies, waits for them, and re-layouts, backward_tile(): jnp.stack([key_portion.reshape(rows, kv_heads * HEAD_SIZE), value_portion...  8.77 us
    dot_general x1, matrix products, body(): lax.dot_general(lax.all_gather(out_grad, 'mp', axis=1, tiled=True), w_out...  7.82 us
    unnamed x59, local copies, waits for them, and re-layouts  7.78 us
    dot_general x4, matrix products, backward_tile(): jnp.einsum('hgqk,qhgd->khd', probs.astype(jnp.bfloat16), gradient_quad, p...  6.39 us
    dot_general x4, matrix products, backward_tile(): jnp.einsum('qhgd,khd->hgqk', gradient_quad, value_slab, preferred_element...  5.03 us
    dot_general x4, matrix products, capped(): jnp.einsum('qhgd,khd->hgqk', query_quad, key_slab, preferred_element_type...  4.67 us
  transfers between devices with their start and end apart: 10, of which 6 were waited for; matrix products, arithmetic and copies ran while one was open for 17% of the time, Pallas kernels for 0%

commit v1 on v0

v1 whole, which is shorter than its diff:
```python
import functools

import jax
import jax.numpy as jnp
from jax import lax
from jax.experimental import pallas as pl
from jax.experimental.pallas import tpu as pltpu
from jax.sharding import PartitionSpec as P

QUERY_HEADS = 32
KEY_VALUE_HEADS = 16
HEAD_SIZE = 128
SPAN = 4
GROUPS = QUERY_HEADS // KEY_VALUE_HEADS
CAP = 50.0
SCALE = 1.0 / 12.0

NN = (((1,), (0,)), ((), ()))
NT = (((1,), (1,)), ((), ()))
TN = (((0,), (0,)), ((), ()))


def dot(a, b, dims):
    return lax.dot_general(a, b, dims, preferred_element_type=jnp.float32)


def kernel(
    n, m, heads, rows, width,
    ids_ref, q_ref, k_ref, v_ref, og_ref, w_ref,
    dq_ref, dk_ref, dv_ref,
    kv, og, wv, qb, hacc, hgt, ids, mask, ubuf, wbuf, acc, tot, grad, back, dqb, fin,
    sem_kv, sem_q, sem_og, sem_w, sem_out,
    ids_s, ids_r, fwd_s, fwd_r, ret_s, ret_r, og_s, og_r,
):
    i = lax.axis_index("ctx")
    me = lax.axis_index("mp")
    odd = lax.rem(i, 2) == 1
    even = lax.rem(i, 2) == 0
    chips = m // 2
    partner = me + 1 - 2 * lax.rem(me, 2)
    d = HEAD_SIZE

    def near(step):
        return {"ctx": lax.rem(i + step + n, n)}

    def load_kv(h, part):
        src = k_ref if part == 0 else v_ref
        return pltpu.make_async_copy(src.at[:, pl.ds(h * d, d)], kv.at[0, h, part], sem_kv.at[h, part])

    def load_q(h, g):
        return pltpu.make_async_copy(
            q_ref.at[:, pl.ds((h * GROUPS + g) * d, d)], qb.at[h, pl.ds(g * rows, rows)], sem_q.at[h, g]
        )

    load_og = pltpu.make_async_copy(og_ref, og.at[me], sem_og)

    def load_w(s):
        if width % 128:
            src = w_ref.at[s]
        else:
            src = w_ref.at[:, pl.ds(s * width, width)]
        return pltpu.make_async_copy(src, wv.at[s], sem_w.at[s])

    load_og.start()
    for h in range(heads):
        for part in range(2):
            load_kv(h, part).start()
    for s in range(m):
        load_w(s).start()
    for h in range(heads):
        for g in range(GROUPS):
            load_q(h, g).start()

    barrier = pltpu.get_barrier_semaphore()
    count = m - 1
    for step in range(1, m):
        pl.semaphore_signal(barrier, inc=1, device_id={"mp": lax.rem(me + step, m)}, device_id_type=pl.DeviceIdType.MESH)
    for step in range(1, SPAN):
        for sign in (1, -1):
            there = (i + step < n) if sign == 1 else (i >= step)

            @pl.when(there)
            def _():
                pl.semaphore_signal(barrier, inc=1, device_id=near(sign * step), device_id_type=pl.DeviceIdType.MESH)

            count = count + there.astype(jnp.int32)
    pl.semaphore_wait(barrier, count)

    def remote(src, dst, send, recv, device):
        return pltpu.make_async_remote_copy(
            src_ref=src, dst_ref=dst, send_sem=send, recv_sem=recv, device_id=device,
            device_id_type=pl.DeviceIdType.MESH,
        )

    def send_ids(hop):
        return remote(ids_ref, ids.at[hop - 1], ids_s.at[hop - 1], ids_r.at[hop - 1], near(hop))

    for hop in range(1, SPAN):

        @pl.when(i + hop < n)
        def _():
            send_ids(hop).start()

    def og_across(step):
        return remote(og.at[me], og.at[me], og_s.at[step - 1], og_r.at[step - 1], {"mp": lax.rem(me + 2 * step, m)})

    def og_from(step):
        s = lax.rem(me - 2 * step + m, m)
        return remote(og.at[s], og.at[s], og_s.at[step - 1], og_r.at[step - 1], {"mp": partner})

    def og_pair(step, slot):
        k = chips - 1 + step
        return remote(og.at[slot], og.at[slot], og_s.at[k], og_r.at[k], {"mp": partner})

    load_og.wait()
    for step in range(1, chips):
        og_across(step).start()
    og_pair(0, me).start()

    def two(h):
        return remote(kv.at[0, h], kv.at[2, h], fwd_s.at[0, h], fwd_r.at[0, h], near(2))

    def pair_even(h):
        return remote(kv.at[0, h], kv.at[1, h], fwd_s.at[1, h], fwd_r.at[1, h], near(1))

    def pair_odd(h):
        return remote(kv.at[2, h], kv.at[1, h], fwd_s.at[1, h], fwd_r.at[1, h], near(-1))

    def three(h):
        return remote(kv.at[1, h], kv.at[3, h], fwd_s.at[2, h], fwd_r.at[2, h], near(2))

    for h in range(heads):
        for part in range(2):
            load_kv(h, part).wait()

        @pl.when(i + 2 < n)
        def _():
            two(h).start()

        @pl.when(even)
        def _():
            pair_even(h).start()

    def product(s, first):
        pltpu.make_async_copy(wv.at[s], wv.at[s], sem_w.at[s]).wait()
        half = 4 * d if (heads * GROUPS) % 4 == 0 else d

        def rows_of(r, c):
            at = pl.ds(pl.multiple_of(r * half, half), half)
            part = dot(wv[s, at, :], og[s], NT)
            if first:
                hacc[at, :] = part
            else:
                hacc[at, :] += part
            return c

        lax.fori_loop(0, heads * GROUPS * d // half, rows_of, 0)

    product(me, True)
    og_pair(0, partner).wait_recv()
    product(partner, False)

    for hop in range(1, SPAN):

        @pl.when(i >= hop)
        def _():
            send_ids(hop).wait_recv()

    hops = jnp.minimum(i, SPAN - 1) + 1
    down = lax.broadcasted_iota(jnp.int32, (rows, rows), 0)
    along = lax.broadcasted_iota(jnp.int32, (rows, rows), 1)
    own_ids = ids_ref[0:1, :].astype(jnp.float32)

    def make_mask(hop, row):
        column = jnp.sum(jnp.where(down == along, row, 0.0), axis=1, keepdims=True)
        seen = (column == own_ids) & (down - hop * rows <= along)
        seen = jnp.where(seen, 1.0, 0.0)
        for g in range(GROUPS):
            mask[hop, :, g * rows:(g + 1) * rows] = seen

    make_mask(0, own_ids)
    for hop in range(1, SPAN):

        @pl.when(i >= hop)
        def _():
            make_mask(hop, ids[hop - 1, 0:1, :].astype(jnp.float32))

    for h in range(heads):

        @pl.when(i >= 2)
        def _():
            two(h).wait_recv()

        @pl.when(odd & (i >= 3))
        def _():
            pair_odd(h).start()

        @pl.when(odd | (i >= 2))
        def _():
            pair_even(h).wait_recv()

        @pl.when((i >= 1) & (i + 2 < n))
        def _():
            three(h).start()

    for step in range(1, chips):
        og_from(step).wait_recv()
        og_pair(step, lax.rem(me - 2 * step + m, m)).start()
    for step in range(1, chips):
        product(lax.rem(me - 2 * step + m, m), False)
    for step in range(1, chips):
        s = lax.rem(partner - 2 * step + m, m)
        og_pair(step, s).wait_recv()
        product(s, False)
    for a in range(heads * GROUPS):
        h, g = divmod(a, GROUPS)
        hgt[h, :, g * rows:(g + 1) * rows] = hacc[a * d:(a + 1) * d, :].astype(jnp.bfloat16)
    for h in range(heads):
        for g in range(GROUPS):
            load_q(h, g).wait()

    def put_dq(h, g):
        return pltpu.make_async_copy(
            dqb.at[h, pl.ds(g * rows, rows)], dq_ref.at[:, pl.ds((h * GROUPS + g) * d, d)], sem_q.at[h, g]
        )

    def compute(h):
        q = qb[h]
        acc[...] = jnp.zeros_like(acc)
        tot[...] = jnp.zeros_like(tot)

        def forward(hop, c):
            s = dot(kv[hop, h, 0], q, NT)
            t = jnp.tanh(s * (SCALE / CAP))
            w = jnp.exp(t * CAP) * mask[hop]
            wb = w.astype(jnp.bfloat16)
            wbuf[hop] = wb
            ubuf[hop] = w * (1.0 - t * t)
            tot[...] += jnp.sum(w, axis=0, keepdims=True)
            acc[...] += dot(kv[hop, h, 1], wb, TN)
            return c

        lax.fori_loop(0, hops, forward, 0)
        inverse = 1.0 / tot[0:1, :]
        hg = hgt[h]
        hg32 = hg.astype(jnp.float32)
        delta = jnp.sum(hg32 * acc[...], axis=0, keepdims=True) * inverse
        scaled = (hg32 * inverse).astype(jnp.bfloat16)
        factor = inverse * SCALE
        acc[...] = jnp.zeros_like(acc)

        def backward(hop, c):
            pg = dot(kv[hop, h, 1], hg, NN)
            ds = (ubuf[hop] * ((pg - delta) * factor)).astype(jnp.bfloat16)
            grad[hop, h, 0] = dot(ds, q, NN).astype(jnp.bfloat16)
            grad[hop, h, 1] = dot(wbuf[hop], scaled, NT).astype(jnp.bfloat16)
            acc[...] += dot(kv[hop, h, 0], ds, TN)
            return c

        lax.fori_loop(0, hops, backward, 0)
        dqb[h] = acc[...].T.astype(jnp.bfloat16)

    def from_three(h):
        return remote(grad.at[3, h], back.at[0, h], ret_s.at[0, h], ret_r.at[0, h], near(-2))

    def from_pair(h, step):
        return remote(grad.at[1, h], back.at[1, h], ret_s.at[1, h], ret_r.at[1, h], near(step))

    def from_two(h):
        return remote(grad.at[2, h], back.at[2, h], ret_s.at[2, h], ret_r.at[2, h], near(-2))

    def gather(hop, stage, h):
        total = grad[hop, h].astype(jnp.float32) + back[stage, h].astype(jnp.float32)
        grad[hop, h] = total.astype(jnp.bfloat16)

    def stage_two(h):
        @pl.when((i >= 1) & (i + 2 < n))
        def _():
            from_three(h).wait_recv()
            gather(1, 0, h)

        @pl.when(odd)
        def _():
            from_pair(h, -1).start()

        @pl.when(even & (i >= 2))
        def _():
            from_pair(h, 1).start()

    def stage_three(h):
        @pl.when(odd & (i >= 3))
        def _():
            from_pair(h, 1).wait_recv()
            gather(2, 1, h)
            from_two(h).start()

    def step(h, c):
        @pl.when(i >= 3)
        def _():
            three(h).wait_recv()

        compute(h)

        @pl.when(i >= 3)
        def _():
            from_three(h).start()

        @pl.when(even & (i >= 2))
        def _():
            from_two(h).start()

        for g in range(GROUPS):
            put_dq(h, g).start()

        @pl.when(h >= 1)
        def _():
            stage_two(h - 1)

        @pl.when(h >= 2)
        def _():
            stage_three(h - 2)

        return c

    lax.fori_loop(0, heads, step, 0)
    stage_two(heads - 1)

    def put(h, part):
        dst = dk_ref if part == 0 else dv_ref
        return pltpu.make_async_copy(fin.at[h, part], dst.at[:, pl.ds(h * d, d)], sem_out.at[h, part])

    def finish(h):
        @pl.when(i + 2 < n)
        def _():
            from_two(h).wait_recv()

        @pl.when(even)
        def _():
            from_pair(h, 1).wait_recv()

        total = grad[0, h].astype(jnp.float32)
        total = total + jnp.where(i + 2 < n, back[2, h].astype(jnp.float32), 0.0)
        total = total + jnp.where(even, back[1, h].astype(jnp.float32), 0.0)
        fin[h] = total.astype(jnp.bfloat16)
        for part in range(2):
            put(h, part).start()

    if heads >= 2:
        stage_three(heads - 2)
    stage_three(heads - 1)


    for h in range(heads):
        finish(h)

    for h in range(heads):
        for g in range(GROUPS):
            put_dq(h, g).wait()
        for part in range(2):
            put(h, part).wait()

        @pl.when(i + 2 < n)
        def _():
            two(h).wait_send()

        @pl.when(even | (i >= 3))
        def _():
            pair_even(h).wait_send()

        @pl.when((i >= 1) & (i + 2 < n))
        def _():
            three(h).wait_send()

        @pl.when(i >= 3)
        def _():
            from_three(h).wait_send()

        @pl.when(odd | (i >= 2))
        def _():
            from_pair(h, 1).wait_send()

        @pl.when(i >= 2)
        def _():
            from_two(h).wait_send()

    for hop in range(1, SPAN):

        @pl.when(i + hop < n)
        def _():
            send_ids(hop).wait_send()

    for stp in range(1, chips):
        og_across(stp).wait_send()
    for stp in range(chips):
        og_pair(stp, me).wait_send()


def body(n, m, queries, keys, values, out_grad, doc_ids, w_out):
    rows = queries.shape[0]
    heads = keys.shape[1] // HEAD_SIZE
    width = out_grad.shape[1]
    d = HEAD_SIZE
    wide = GROUPS * rows
    chips = m // 2
    any_space = pl.BlockSpec(memory_space=pl.ANY)
    bf, f32 = jnp.bfloat16, jnp.float32
    dma = pltpu.SemaphoreType.DMA
    w_rows = w_out.shape[0]
    if width % 128:
        w_out = jnp.transpose(w_out.reshape(w_rows, m, width), (1, 0, 2))
    ids = jnp.broadcast_to(doc_ids[None, :], (8, rows))
    return pl.pallas_call(
        functools.partial(kernel, n, m, heads, rows, width),
        out_shape=(
            jax.ShapeDtypeStruct(queries.shape, bf),
            jax.ShapeDtypeStruct(keys.shape, bf),
            jax.ShapeDtypeStruct(values.shape, bf),
        ),
        in_specs=[pl.BlockSpec(memory_space=pltpu.VMEM)] + [any_space] * 5,
        out_specs=(any_space,) * 3,
        scratch_shapes=[
            pltpu.VMEM((SPAN, heads, 2, rows, d), bf),
            pltpu.VMEM((m, rows, width), bf),
            pltpu.VMEM((m, w_rows, width), bf),
            pltpu.VMEM((heads, wide, d), bf),
            pltpu.VMEM((heads * GROUPS * d, rows), f32),
            pltpu.VMEM((heads, d, wide), bf),
            pltpu.VMEM((SPAN - 1, 8, rows), jnp.int32),
            pltpu.VMEM((SPAN, rows, wide), f32),
            pltpu.VMEM((SPAN, rows, wide), f32),
            pltpu.VMEM((SPAN, rows, wide), bf),
            pltpu.VMEM((d, wide), f32),
            pltpu.VMEM((1, wide), f32),
            pltpu.VMEM((SPAN, heads, 2, rows, d), bf),
            pltpu.VMEM((3, heads, 2, rows, d), bf),
            pltpu.VMEM((heads, wide, d), bf),
            pltpu.VMEM((heads, 2, rows, d), bf),
            dma((heads, 2)),
            dma((heads, GROUPS)),
            dma,
            dma((m,)),
            dma((heads, 2)),
            dma((SPAN - 1,)),
            dma((SPAN - 1,)),
            dma((3, heads)),
            dma((3, heads)),
            dma((3, heads)),
            dma((3, heads)),
            dma((2 * chips - 1,)),
            dma((2 * chips - 1,)),
        ],
        compiler_params=pltpu.CompilerParams(
            collective_id=0, has_side_effects=True, vmem_limit_bytes=60 * 1024 * 1024
        ),
    )(ids, queries, keys, values, out_grad, w_out)


def solution(mesh):
    placed = (
        P("ctx", "mp"),
        P("ctx", "mp"),
        P("ctx", "mp"),
        P("ctx", "mp"),
        P("ctx"),
        P("mp", None),
    )
    return jax.shard_map(
        functools.partial(body, mesh.shape["ctx"], mesh.shape["mp"]),
        mesh=mesh,
        in_specs=placed,
        out_specs=(P("ctx", "mp"), P("ctx", "mp"), P("ctx", "mp")),
        check_vma=False,
    )
```

time: 157 us -> 70 us (0.45)
  Pallas kernels: 0 us -> 62.6 us
  waiting for transfers between devices: 48.8 us -> 0 us
  matrix products: 33.7 us -> 0 us
  starting transfers between devices: 29.9 us -> 0 us
  local copies, waits for them, and re-layouts: 21.9 us -> 6.48 us
  between operations: 14.6 us -> 0.64 us
  other arithmetic: 6.78 us -> 0 us
    pallas_call x0 -> x1, Pallas kernels: none -> 62.6 us  [body(): pl.pallas_call(functools.partial(kernel, n, m, heads, rows, width), out_s...]
    ppermute x9 -> x0, waiting for transfers between devices: 48.8 us -> none  [passed_along(): lax.ppermute(value, axis, [(source, source + steps) for source in range(f...]
    dot_general x25 -> x0, matrix products: 33.7 us -> none  [the longest x1 7.82 us: body(): lax.dot_general(lax.all_gather(out_grad, 'mp', axis=1, tiled=True), w_out...]
    ppermute x9 -> x0, starting transfers between devices: 29.9 us -> none  [passed_along(): lax.ppermute(value, axis, [(source, source + steps) for source in range(f...]
    another operation x12 -> x0, local copies, waits for them, and re-layouts: 9.25 us -> none  [the longest x8 8.77 us: backward_tile(): jnp.stack([key_portion.reshape(rows, kv_heads * HEAD_SIZE), value_portion...]
    another operation x5 -> x0, other arithmetic: 6.31 us -> none  [the longest x3 4.61 us: backward_tile(): jnp.stack([key_portion.reshape(rows, kv_heads * HEAD_SIZE), value_portion...]
    unnamed x59 -> x3, local copies, waits for them, and re-layouts: 7.78 us -> 5.21 us
    reshape x2 -> x0, local copies, waits for them, and re-layouts: 2.24 us -> none  [the longest x1 2.04 us: body(): incoming_gradient.reshape(rows, kv_heads, query_groups, HEAD_SIZE)]
  transfers between devices with their start and end apart: 10 -> 0, of which waited for: 6 -> 0; matrix products, arithmetic and copies ran while one was open for 17% -> 0% of each run, Pallas kernels for 0% -> 0%
where the time goes in v1:
time: 70 us; the launch traced here: 69.7 us
  Pallas kernels  62.6 us (89%)
  local copies, waits for them, and re-layouts  6.48 us (9%)
    pallas_call x1, Pallas kernels, body(): pl.pallas_call(functools.partial(kernel, n, m, heads, rows, width), out_s...  62.6 us
    unnamed x3, local copies, waits for them, and re-layouts  5.21 us

profile of v1, /device:TPU:6, one launch (start us, length us, event | category | flops | bytes accessed | tf_op | source)
XLA Modules:
  0.0 69.7 jit_solution(13822930698767186454)
XLA Ops:
  0.6 1.3 %broadcast_in_dim.2.ids_ref = s32[8,256]{1,0:T(8,128)} broadcast(s32[256]{0:T(256)} %param.10), dimensions={1} | broadcast | bytes 9216 | tf_op jit(solution)/shard_map/broadcast_in_dim | solution.py:411
  1.9 62.6 %shard_map.85 = (bf16[256,1024]{1,0:T(8,128)(2,1)}, bf16[256,512]{1,0:T(8,128)(2,1)}, bf16[256,512]{1,0:T(8,128)(2,1)}) custom-call(s32[8,256]{1,0:T(8,128)} %broadcast_in_dim.2.ids_ref, bf16[256,1024]{1,0:T(8,128)(2,1)} %q_ref.1, bf16[256,512]{1,0:T(8,128)(2,1)} %k_ref.1, bf16[256,512]{1,0:T(8,128)(2,1)} %v_ref.1, bf16[256,1152]{1,0:T(8,128)(2,1)} %og_ref.1, ...), custom_call_target="tpu_custom_call" | custom-call | tf_op jit(solution)/shard_map/pallas_call | solution.py:412
  64.5 1.9 %copy.12 = bf16[256,1024]{1,0:T(8,128)(2,1)} copy(bf16[256,1024]{1,0:T(8,128)(2,1)} %get-tuple-element.6) | data formatting | bytes 1048576
  66.4 1.7 %copy.13 = bf16[256,512]{1,0:T(8,128)(2,1)} copy(bf16[256,512]{1,0:T(8,128)(2,1)} %get-tuple-element.7) | data formatting | bytes 524288
  68.0 1.7 %copy.14 = bf16[256,512]{1,0:T(8,128)(2,1)} copy(bf16[256,512]{1,0:T(8,128)(2,1)} %get-tuple-element.8) | data formatting | bytes 524288

commit v2 on v1

--- a/solution.py
+++ b/solution.py
@@ -93,7 +93,7 @@
         )
 
     def send_ids(hop):
-        return remote(ids_ref, ids.at[hop - 1], ids_s.at[hop - 1], ids_r.at[hop - 1], near(hop))
+        return remote(ids_ref, ids[hop - 1], ids_s.at[hop - 1], ids_r.at[hop - 1], near(hop))
 
     for hop in range(1, SPAN):
 
@@ -129,13 +129,19 @@
     def three(h):
         return remote(kv.at[1, h], kv.at[3, h], fwd_s.at[2, h], fwd_r.at[2, h], near(2))
 
+    early = max(heads - 1, 1)
+
+    def send_two(h):
+        @pl.when(i + 2 < n)
+        def _():
+            two(h).start()
+
     for h in range(heads):
         for part in range(2):
             load_kv(h, part).wait()
 
-        @pl.when(i + 2 < n)
-        def _():
-            two(h).start()
+        if h < early:
+            send_two(h)
 
         @pl.when(even)
         def _():
@@ -169,7 +175,7 @@
     hops = jnp.minimum(i, SPAN - 1) + 1
     down = lax.broadcasted_iota(jnp.int32, (rows, rows), 0)
     along = lax.broadcasted_iota(jnp.int32, (rows, rows), 1)
-    own_ids = ids_ref[0:1, :].astype(jnp.float32)
+    own_ids = ids_ref[...].reshape(1, rows).astype(jnp.float32)
 
     def make_mask(hop, row):
         column = jnp.sum(jnp.where(down == along, row, 0.0), axis=1, keepdims=True)
@@ -183,10 +189,9 @@
 
         @pl.when(i >= hop)
         def _():
-            make_mask(hop, ids[hop - 1, 0:1, :].astype(jnp.float32))
-
-    for h in range(heads):
-
+            make_mask(hop, ids[hop - 1][...].reshape(1, rows).astype(jnp.float32))
+
+    def relay(h):
         @pl.when(i >= 2)
         def _():
             two(h).wait_recv()
@@ -203,28 +208,20 @@
         def _():
             three(h).start()
 
-    for step in range(1, chips):
-        og_from(step).wait_recv()
-        og_pair(step, lax.rem(me - 2 * step + m, m)).start()
-    for step in range(1, chips):
-        product(lax.rem(me - 2 * step + m, m), False)
-    for step in range(1, chips):
-        s = lax.rem(partner - 2 * step + m, m)
-        og_pair(step, s).wait_recv()
-        product(s, False)
-    for a in range(heads * GROUPS):
-        h, g = divmod(a, GROUPS)
-        hgt[h, :, g * rows:(g + 1) * rows] = hacc[a * d:(a + 1) * d, :].astype(jnp.bfloat16)
-    for h in range(heads):
-        for g in range(GROUPS):
-            load_q(h, g).wait()
+        if h == 0:
+            for later in range(early, heads):
+                send_two(later)
 
     def put_dq(h, g):
         return pltpu.make_async_copy(
             dqb.at[h, pl.ds(g * rows, rows)], dq_ref.at[:, pl.ds((h * GROUPS + g) * d, d)], sem_q.at[h, g]
         )
 
-    def compute(h):
+    def forward_pass(h):
+        @pl.when(i >= 3)
+        def _():
+            three(h).wait_recv()
+
         q = qb[h]
         acc[...] = jnp.zeros_like(acc)
         tot[...] = jnp.zeros_like(tot)
@@ -241,6 +238,9 @@
             return c
 
         lax.fori_loop(0, hops, forward, 0)
+
+    def backward_pass(h):
+        q = qb[h]
         inverse = 1.0 / tot[0:1, :]
         hg = hgt[h]
         hg32 = hg.astype(jnp.float32)
@@ -259,6 +259,8 @@
 
         lax.fori_loop(0, hops, backward, 0)
         dqb[h] = acc[...].T.astype(jnp.bfloat16)
+        for g in range(GROUPS):
+            put_dq(h, g).start()
 
     def from_three(h):
         return remote(grad.at[3, h], back.at[0, h], ret_s.at[0, h], ret_r.at[0, h], near(-2))
@@ -294,35 +296,62 @@
             gather(2, 1, h)
             from_two(h).start()
 
+    def send_back(h):
+        @pl.when(i >= 3)
+        def _():
+            from_three(h).start()
+
+        @pl.when(even & (i >= 2) & (h != heads - 2))
+        def _():
+            from_two(h).start()
+
+        @pl.when(even & (i >= 2) & (h == heads - 1) & (h >= 1))
+        def _():
+            from_two(heads - 2).start()
+
     def step(h, c):
-        @pl.when(i >= 3)
-        def _():
-            three(h).wait_recv()
-
-        compute(h)
-
-        @pl.when(i >= 3)
-        def _():
-            from_three(h).start()
-
-        @pl.when(even & (i >= 2))
-        def _():
-            from_two(h).start()
-
+        backward_pass(h)
+        send_back(h)
+
+        @pl.when(h + 1 < heads)
+        def _():
+            forward_pass(h + 1)
+
+        stage_two(h - 1)
+
+        @pl.when(h >= 2)
+        def _():
+            stage_three(h - 2)
+
+        return c
+
+    for h in range(early):
+        relay(h)
+    for h in range(heads):
         for g in range(GROUPS):
-            put_dq(h, g).start()
-
-        @pl.when(h >= 1)
-        def _():
-            stage_two(h - 1)
-
-        @pl.when(h >= 2)
-        def _():
-            stage_three(h - 2)
-
-        return c
-
-    lax.fori_loop(0, heads, step, 0)
+            load_q(h, g).wait()
+    for step_ in range(1, chips):
+        og_from(step_).wait_recv()
+        og_pair(step_, lax.rem(me - 2 * step_ + m, m)).start()
+    for step_ in range(1, chips):
+        product(lax.rem(me - 2 * step_ + m, m), False)
+    forward_pass(0)
+    for step_ in range(1, chips):
+        s = lax.rem(partner - 2 * step_ + m, m)
+        og_pair(step_, s).wait_recv()
+        product(s, False)
+    for a in range(heads * GROUPS):
+        h, g = divmod(a, GROUPS)
+        hgt[h, :, g * rows:(g + 1) * rows] = hacc[a * d:(a + 1) * d, :].astype(jnp.bfloat16)
+    backward_pass(0)
+    send_back(0)
+    if heads > 2:
+        forward_pass(1)
+    for h in range(early, heads):
+        relay(h)
+    if heads == 2:
+        forward_pass(1)
+    lax.fori_loop(1, heads, step, 0)
     stage_two(heads - 1)
 
     def put(h, part):
@@ -393,6 +422,12 @@
         og_across(stp).wait_send()
     for stp in range(chips):
         og_pair(stp, me).wait_send()
+
+
+def put_out(a_ref, b_ref, c_ref, x_ref, y_ref, z_ref):
+    x_ref[...] = a_ref[...]
+    y_ref[...] = b_ref[...]
+    z_ref[...] = c_ref[...]
 
 
 def body(n, m, queries, keys, values, out_grad, doc_ids, w_out):
@@ -408,8 +443,7 @@
     w_rows = w_out.shape[0]
     if width % 128:
         w_out = jnp.transpose(w_out.reshape(w_rows, m, width), (1, 0, 2))
-    ids = jnp.broadcast_to(doc_ids[None, :], (8, rows))
-    return pl.pallas_call(
+    results = pl.pallas_call(
         functools.partial(kernel, n, m, heads, rows, width),
         out_shape=(
             jax.ShapeDtypeStruct(queries.shape, bf),
@@ -425,7 +459,7 @@
             pltpu.VMEM((heads, wide, d), bf),
             pltpu.VMEM((heads * GROUPS * d, rows), f32),
             pltpu.VMEM((heads, d, wide), bf),
-            pltpu.VMEM((SPAN - 1, 8, rows), jnp.int32),
+            [pltpu.VMEM((rows,), jnp.int32)] * (SPAN - 1),
             pltpu.VMEM((SPAN, rows, wide), f32),
             pltpu.VMEM((SPAN, rows, wide), f32),
             pltpu.VMEM((SPAN, rows, wide), bf),
@@ -452,7 +486,17 @@
         compiler_params=pltpu.CompilerParams(
             collective_id=0, has_side_effects=True, vmem_limit_bytes=60 * 1024 * 1024
         ),
-    )(ids, queries, keys, values, out_grad, w_out)
+    )(doc_ids, queries, keys, values, out_grad, w_out)
+
+    blocks = 2
+    specs = [pl.BlockSpec((rows // blocks, r.shape[1]), lambda b: (b, 0)) for r in results]
+    return pl.pallas_call(
+        put_out,
+        grid=(blocks,),
+        out_shape=tuple(jax.ShapeDtypeStruct(r.shape, bf) for r in results),
+        in_specs=specs,
+        out_specs=tuple(specs),
+    )(*results)
 
 
 def solution(mesh):

time: 70 us -> 61.4 us (0.88); the launches traced: 69.7 us -> 60.3 us
  local copies, waits for them, and re-layouts: 6.48 us -> 0 us
  Pallas kernels: 62.6 us -> 59.6 us
    unnamed x3 -> x0, local copies, waits for them, and re-layouts: 5.21 us -> none
    pallas_call x1, Pallas kernels: 62.6 us -> 57.6 us  [body(): pl.pallas_call(functools.partial(kernel, n, m, heads, rows, width), out_s...]
    pallas_call x0 -> x1, Pallas kernels: none -> 2.08 us  [body(): pl.pallas_call(put_out, grid=(blocks,), out_shape=tuple((jax.ShapeDtypeSt...]
    broadcast_in_dim x1 -> x0, local copies, waits for them, and re-layouts: 1.28 us -> none  [body(): ids = jnp.broadcast_to(doc_ids[None, :], (8, rows))]
where the time goes in v2:
time: 61.4 us; the launch traced here: 60.3 us
  Pallas kernels  59.6 us (97%)
  between operations  0.64 us (1%)
    pallas_call x1, Pallas kernels, body(): pl.pallas_call(functools.partial(kernel, n, m, heads, rows, width), out_s...  57.6 us
    pallas_call x1, Pallas kernels, body(): pl.pallas_call(put_out, grid=(blocks,), out_shape=tuple((jax.ShapeDtypeSt...  2.08 us

profile of v2, /device:TPU:6, one launch (start us, length us, event | category | flops | bytes accessed | tf_op | source)
XLA Modules:
  0.0 60.3 jit_solution(5573282608732714976)
XLA Ops:
  0.6 57.6 %shard_map.85 = (bf16[256,1024]{1,0:T(8,128)(2,1)}, bf16[256,512]{1,0:T(8,128)(2,1)}, bf16[256,512]{1,0:T(8,128)(2,1)}) custom-call(s32[256]{0:T(256)} %ids_ref.1, bf16[256,1024]{1,0:T(8,128)(2,1)} %q_ref.1, bf16[256,512]{1,0:T(8,128)(2,1)} %k_ref.1, bf16[256,512]{1,0:T(8,128)(2,1)} %v_ref.1, bf16[256,1152]{1,0:T(8,128)(2,1)} %og_ref.1, bf16[1024,4608]{1,0:T(8,128)(2,1)} %w_ref.1), custom_call_target="tpu_custom_call" | custom-call | tf_op jit(solution)/shard_map/pallas_call | solution.py:446
  58.2 2.1 %shard_map.86 = (bf16[256,1024]{1,0:T(8,128)(2,1)}, bf16[256,512]{1,0:T(8,128)(2,1)}, bf16[256,512]{1,0:T(8,128)(2,1)}) custom-call(bf16[256,1024]{1,0:T(8,128)(2,1)} %get-tuple-element.6.a_ref, bf16[256,512]{1,0:T(8,128)(2,1)} %get-tuple-element.7.b_ref, bf16[256,512]{1,0:T(8,128)(2,1)} %get-tuple-element.8.c_ref), custom_call_target="tpu_custom_call" | custom-call | tf_op jit(solution)/shard_map/pallas_call | solution.py:493
